TPU v7x, 512 devices: a whole 4x4x16 slice. The times are simulated.
512 devices in a mesh: egrp: 32 (over x, z_hi, core), eloc: 16 (over y, z_lo).
Axes of the slice: x: 4, y: 4, z: 16 (z_hi: 4, z_lo: 4; z = z_hi * 4 + z_lo), core: 2. Of those that a mesh axis runs over, the one named last changes fastest.
Arguments:
- green_blocks: bfloat16 [512, 16, 3, 64, 128], P(('egrp', 'eloc')), may hold values from -0.3125 to 0.3125
- sigma_prev: bfloat16 [512, 16, 64, 128], P(('egrp', 'eloc')), may hold values from -6 to 6
- neighbours: int32 [16, 2], replicated, may hold values from 0 to 15
- couplings: bfloat16 [6, 16, 64, 128], P(None, 'eloc'), may hold values from -0.375 to 0.375
- occupancy: float32 [6], replicated, may hold values from 0.1 to 2
- shifts: int32 [6], replicated, may hold values from 1 to 16, as said below
Outputs:
- sigma_next: bfloat16 [512, 16, 64, 128], P(('egrp', 'eloc'))
Inputs may be any that keep to these rules, and one draw needn't show every extreme that they name: `shifts`: at least one mode's shift equals 16.
All inputs are finite; a program needn't handle non-finite values.
Results may differ from a plain program's by a relative error of at most 0.0065.
Values may be sent and summed in bfloat16 or wider, within the bound.
A program may use at most 64 MiB of HBM per device.

v0:
```python
import jax
import jax.numpy as jnp
from jax import lax
from jax.sharding import PartitionSpec as P


def extended_2(cells, sides, width):
    for axis, dim in sides:
        count = lax.axis_size(axis)
        ends = count - 1
        head = lax.slice_in_dim(cells, 0, width, axis=dim)
        tail = lax.slice_in_dim(cells, cells.shape[dim] - width, cells.shape[dim], axis=dim)
        cells = jnp.concatenate(
            [
                lax.ppermute(tail, axis, [(i, (i + 1) % count) for i in range(ends)]),
                cells,
                lax.ppermute(head, axis, [((i + 1) % count, i) for i in range(ends)]),
            ],
            axis=dim,
        )
    return cells


def widened_form(block):
    orbitals = block.shape[-2]
    real_part = block[..., :orbitals]
    imag_part = block[..., orbitals:]
    upper_rows = jnp.concatenate([real_part, imag_part], -1)
    lower_rows = jnp.concatenate([-imag_part, real_part], -1)
    return jnp.concatenate([upper_rows, lower_rows], -2)


def adjoint_form(block):
    orbitals = block.shape[-2]
    real_part = jnp.swapaxes(block[..., :orbitals], -1, -2)
    imag_part = jnp.swapaxes(block[..., orbitals:], -1, -2)
    upper_rows = jnp.concatenate([real_part, -imag_part], -1)
    lower_rows = jnp.concatenate([imag_part, real_part], -1)
    return jnp.concatenate([upper_rows, lower_rows], -2)


def shards(green_blocks, sigma_prev, neighbours, couplings, occupancy, shifts):
    blocks = green_blocks[0]
    sigma_local = sigma_prev[0]
    atom_count = blocks.shape[0]
    atom_index = jnp.concatenate([jnp.arange(atom_count, dtype=jnp.int32)[:, None], neighbours], 1)
    chosen = jnp.take(sigma_local, atom_index, axis=0)
    half_product = jnp.einsum(
        "akij,akjl->akil", blocks, widened_form(chosen), preferred_element_type=jnp.float32
    ).astype(jnp.bfloat16)
    lesser = jnp.einsum(
        "akij,akjl->ail", half_product, adjoint_form(blocks), preferred_element_type=jnp.float32
    )
    regrouped = lax.all_to_all(
        lesser[None].astype(jnp.bfloat16), "eloc", split_axis=1, concat_axis=0, tiled=True
    ).astype(jnp.float32)
    group_size = regrouped.shape[0]
    mode_count = couplings.shape[0]
    coupling_float = couplings.astype(jnp.float32)
    right_forms = adjoint_form(coupling_float)
    extended = extended_2(regrouped.astype(jnp.bfloat16), (("egrp", 0),), group_size).astype(
        regrouped.dtype
    )
    self_energy = jnp.zeros_like(regrouped)
    for mode_index in range(mode_count):
        shift_now = shifts[mode_index]
        upper_part = lax.dynamic_slice_in_dim(extended, group_size + shift_now, group_size, 0)
        lower_part = lax.dynamic_slice_in_dim(extended, group_size - shift_now, group_size, 0)
        mixture = (occupancy[mode_index] + 1.0) * upper_part + occupancy[mode_index] * lower_part
        left = jnp.einsum(
            "aij,eajl->eail",
            coupling_float[mode_index],
            widened_form(mixture),
            precision=lax.Precision.HIGHEST,
        )
        self_energy = self_energy + jnp.einsum(
            "eaij,ajl->eail", left, right_forms[mode_index], precision=lax.Precision.HIGHEST
        )
    result = self_energy.astype(jnp.bfloat16)
    return lax.all_to_all(result, "eloc", split_axis=0, concat_axis=1, tiled=True)


def solution(mesh):
    return jax.shard_map(
        shards,
        mesh=mesh,
        in_specs=(
            P(("egrp", "eloc"), None, None, None, None),
            P(("egrp", "eloc"), None, None, None),
            P(),
            P(None, "eloc", None, None),
            P(),
            P(),
        ),
        out_specs=P(("egrp", "eloc"), None, None, None),
        check_vma=False,
    )
```

profile of v0, /device:TPU:5, one launch (start us, length us, event | category | flops | bytes accessed | tf_op | source)
XLA Modules:
  0.0 99.2 jit_solution(8592117828195106142)
XLA Ops:
  0.0 0.0 copy-start
  0.0 0.7 compare_select_fusion
  0.7 0.1 copy.17
  0.8 0.1 reshape.301
  0.9 0.7 compare_and_fusion
  1.6 0.1 copy.16
  1.7 1.8 %copy.18 = bf16[1,16,3,64,128]{3,4,2,1,0:T(8,128)(2,1)S(1)} copy(bf16[1,16,3,64,128]{4,3,2,1,0:T(8,128)(2,1)} %param.6) | data formatting | bytes 1572864 | tf_op args[0]
  3.5 1.3 %slice_bitcast_fusion = (bf16[16,3,64,64]{3,2,1,0:T(8,128)(2,1)}, bf16[16,3,64,64]{3,2,1,0:T(8,128)(2,1)}) fusion(bf16[16,3,64,128]{2,3,1,0:T(8,128)(2,1)S(1)} %bitcast.196), kind=kLoop, calls=%fused_computation.63 | loop fusion | bytes 1572864 | tf_op jit(solution)/shard_map/transpose | solution.py:36
  4.8 0.0 copy-done
  4.8 0.7 gather_fusion
  5.5 0.1 broadcast_select_fusion
  5.7 1.5 %slice_negate_fusion = (bf16[16,3,64,64]{3,2,1,0:T(8,128)(2,1)S(1)}, bf16[16,3,64,64]{3,2,1,0:T(8,128)(2,1)}, bf16[16,3,64,64]{3,2,1,0:T(8,128)(2,1)}) fusion(bf16[16,3,64,128]{3,2,1,0:T(8,128)(2,1)S(1)} %broadcast_select_fusion, bf16[16,3,64,128]{2,3,1,0:T(8,128)(2,1)S(1)} %bitcast.197), kind=kLoop, calls=%fused_computation.65 | loop fusion | flops 393216 | bytes 2359296 | tf_op jit(solution)/shard_map/neg | solution.py:29
  7.2 4.7 %fusion.28 = bf16[1,16,64,128]{3,2,0,1:T(8,128)(2,1)} fusion(bf16[16,3,64,64]{3,2,1,0:T(8,128)(2,1)} %get-tuple-element.12, bf16[16,3,64,64]{3,2,1,0:T(8,128)(2,1)} %get-tuple-element.11, bf16[16,3,64,64]{3,2,1,0:T(8,128)(2,1)} %get-tuple-element.41, bf16[16,3,64,64]{3,2,1,0:T(8,128)(2,1)} %get-tuple-element.14, ...), kind=kOutput, calls=%fused_computation.32 | convolution fusion | flops 212860928 | bytes 3801088 | tf_op jit(solution)/shard_map/akij,akjl->ail/dot_general | solution.py:51
  11.9 8.4 %all-to-all-start = ((bf16[1,16,64,128]{3,2,0,1:T(8,128)(2,1)}), bf16[1,16,64,128]{3,2,0,1:T(8,128)(2,1)S(1)}, u32[]{:S(2)}, u32[]{:S(2)}) async-start(bf16[1,16,64,128]{3,2,0,1:T(8,128)(2,1)} %fusion.28), calls=%async_computation | async-start | bytes 524288 | tf_op jit(solution)/shard_map/all_to_all | solution.py:54
  20.3 0.0 copy-done.2
  20.3 0.7 fusion.83
  35.8 0.0 copy-done.3
  35.8 0.7 fusion.82
  40.1 0.2 copy.15
  40.5 0.0 all-to-all-done
  40.5 9.7 %collective-permute-start = (bf16[16,1,64,128]{3,2,0,1:T(8,128)(2,1)S(1)}, bf16[16,1,64,128]{3,2,0,1:T(8,128)(2,1)S(1)}, u32[]{:S(2)}, u32[]{:S(2)}) collective-permute-start(bf16[16,1,64,128]{3,2,0,1:T(8,128)(2,1)S(1)} %bitcast.199), channel_id=1, source_target_pairs={{0,16},{16,32},{32,48},{48,64},{64,80},{80,96},{96,112},{112,128},... | collective-permute-start | bytes 786440 | tf_op jit(solution)/shard_map/ppermute | solution.py:15
  50.2 2.1 %collective-permute-start.1 = (bf16[16,1,64,128]{3,2,0,1:T(8,128)(2,1)S(1)}, bf16[16,1,64,128]{3,2,0,1:T(8,128)(2,1)S(1)}, u32[]{:S(2)}, u32[]{:S(2)}) collective-permute-start(bf16[16,1,64,128]{3,2,0,1:T(8,128)(2,1)S(1)} %bitcast.200), channel_id=1, source_target_pairs={{16,0},{32,16},{48,32},{64,48},{80,64},{96,80},{112,96},{128,112},... | collective-permute-start | bytes 786440 | tf_op jit(solution)/shard_map/ppermute | solution.py:17
  52.3 0.2 maximum_maximum_fusion
  52.5 1.3 %collective-permute-done = bf16[16,1,64,128]{3,2,0,1:T(8,128)(2,1)S(1)} collective-permute-done((bf16[16,1,64,128]{3,2,0,1:T(8,128)(2,1)S(1)}, bf16[16,1,64,128]{3,2,0,1:T(8,128)(2,1)S(1)}, u32[]{:S(2)}, u32[]{:S(2)}) %collective-permute-start) | collective-permute-done | bytes 262176 | tf_op jit(solution)/shard_map/ppermute | solution.py:15
  53.7 11.2 %collective-permute-done.1 = bf16[16,1,64,128]{3,2,0,1:T(8,128)(2,1)S(1)} collective-permute-done((bf16[16,1,64,128]{3,2,0,1:T(8,128)(2,1)S(1)}, bf16[16,1,64,128]{3,2,0,1:T(8,128)(2,1)S(1)}, u32[]{:S(2)}, u32[]{:S(2)}) %collective-permute-start.1) | collective-permute-done | bytes 262176 | tf_op jit(solution)/shard_map/ppermute | solution.py:17
  65.0 0.1 maximum_convert_fusion
  65.1 3.1 %multiply_add_fusion = (f32[16,1,64,128]{3,2,0,1:T(8,128)S(1)}, f32[16,1,64,128]{3,2,0,1:T(8,128)S(1)}, f32[16,1,64,128]{3,2,0,1:T(8,128)S(1)}, f32[16,1,64,128]{3,2,0,1:T(8,128)S(1)}) fusion(f32[48,1,64,128]{3,2,0,1:T(8,128)S(1)} %maximum_convert_fusion, s32[]{:T(128)S(6)} %select_n.70, s32[]{:T(128)S(6)} %select_n.69, f32[]{:T(128)} %bitcast.82, ...), kind=kLoop, calls=%fused_computation.75 | loop fusion | flops 1572864 | bytes 6291520 | tf_op jit(solution)/shard_map/add | solution.py:69
  68.2 0.2 slice_negate_fusion.1
  68.4 1.4 %multiply_add_fusion.1 = (f32[16,1,64,128]{3,2,0,1:T(8,128)S(1)}, f32[16,1,64,128]{3,2,0,1:T(8,128)S(1)}) fusion(f32[48,1,64,128]{3,2,0,1:T(8,128)S(1)} %maximum_convert_fusion, s32[]{:T(128)S(6)} %select_n.68, s32[]{:T(128)S(6)} %select_n.67, f32[]{:T(128)} %bitcast.69, f32[]{:T(128)S(6)} %add.243, s32[]{:T(128)S(6)} %select_n.60, f32[]{:T(128)} %bitcast.4, ...), kind=kLoop, calls=%fused_computation.76 | loop fusion | flops 786432 | bytes 3145760 | tf_op jit(solution)/shard_map/add | solution.py:69
  69.8 0.2 slice_negate_fusion.2
  70.0 0.2 slice_negate_fusion.3
  70.3 0.2 slice_negate_fusion.4
  70.5 0.2 slice_negate_fusion.5
  70.7 0.2 slice_negate_fusion.6
  70.9 0.6 convolution_bitcast_fusion
  71.5 0.6 convolution_bitcast_fusion.1
  72.1 0.6 convolution_bitcast_fusion.2
  72.7 0.6 convolution_bitcast_fusion.3
  73.4 0.6 convolution_bitcast_fusion.4
  74.0 0.6 convolution_bitcast_fusion.5
  74.6 0.6 fusion.59
  75.2 0.6 convolution_add_fusion.4
  75.7 0.6 convolution_add_fusion.3
  76.3 0.6 convolution_add_fusion.2
  76.9 0.6 convolution_add_fusion.1
  77.5 0.6 fusion.27
  78.0 20.4 %all_to_all.24 = bf16[16,1,64,128]{3,2,1,0:T(8,128)(2,1)S(1)} all-to-all(bf16[16,1,64,128]{3,2,1,0:T(8,128)(2,1)S(1)} %fusion.27), channel_id=1, replica_groups=mesh['egrp'=32,'eloc'=16] {'eloc'}, dimensions={0} | all-to-all | bytes 524288 | tf_op jit(solution)/shard_map/all_to_all | solution.py:80
  98.5 0.7 copy.27
  (10 shorter events, 0.1 us)
Async XLA Ops:
  0.0 4.8 %copy-start = (bf16[1,16,64,128]{3,2,1,0:T(8,128)(2,1)S(1)}, bf16[1,16,64,128]{3,2,1,0:T(8,128)(2,1)}, u32[]{:S(2)}) copy-start(bf16[1,16,64,128]{3,2,1,0:T(8,128)(2,1)} %param.7) | copy-start | bytes 786436
  7.2 13.1 %copy-start.2 = (s32[6]{0:T(128)S(1)}, s32[6]{0:T(128)}, u32[]{:S(2)}) copy-start(s32[6]{0:T(128)} %param.11) | copy-start | bytes 76
  7.2 28.6 %copy-start.3 = (f32[6]{0:T(128)S(1)}, f32[6]{0:T(128)}, u32[]{:S(2)}) copy-start(f32[6]{0:T(128)} %param.10) | copy-start | bytes 76
  7.2 32.9 %copy-start.1 = (bf16[6,1,64,128]{3,2,1,0:T(8,128)(2,1)S(1)}, bf16[6,1,64,128]{3,2,1,0:T(8,128)(2,1)}, u32[]{:S(2)}) copy-start(bf16[6,1,64,128]{3,2,1,0:T(8,128)(2,1)} %param.9) | copy-start | bytes 294916
  11.9 28.6 %all-to-all-start = ((bf16[1,16,64,128]{3,2,0,1:T(8,128)(2,1)}), bf16[1,16,64,128]{3,2,0,1:T(8,128)(2,1)S(1)}, u32[]{:S(2)}, u32[]{:S(2)}) async-start(bf16[1,16,64,128]{3,2,0,1:T(8,128)(2,1)} %fusion.28), calls=%async_computation | async-start | bytes 524288 | tf_op jit(solution)/shard_map/all_to_all | solution.py:54
  40.5 13.3 %collective-permute-start = (bf16[16,1,64,128]{3,2,0,1:T(8,128)(2,1)S(1)}, bf16[16,1,64,128]{3,2,0,1:T(8,128)(2,1)S(1)}, u32[]{:S(2)}, u32[]{:S(2)}) collective-permute-start(bf16[16,1,64,128]{3,2,0,1:T(8,128)(2,1)S(1)} %bitcast.199), channel_id=1, source_target_pairs={{0,16},{16,32},{32,48},{48,64},{64,80},{80,96},{96,112},{112,128},... | collective-permute-start | bytes 786440 | tf_op jit(solution)/shard_map/ppermute | solution.py:15
  50.2 14.8 %collective-permute-start.1 = (bf16[16,1,64,128]{3,2,0,1:T(8,128)(2,1)S(1)}, bf16[16,1,64,128]{3,2,0,1:T(8,128)(2,1)S(1)}, u32[]{:S(2)}, u32[]{:S(2)}) collective-permute-start(bf16[16,1,64,128]{3,2,0,1:T(8,128)(2,1)S(1)} %bitcast.200), channel_id=1, source_target_pairs={{16,0},{32,16},{48,32},{64,48},{80,64},{96,80},{112,96},{128,112},... | collective-permute-start | bytes 786440 | tf_op jit(solution)/shard_map/ppermute | solution.py:17
where the time goes:
time: 99.8 us; the launch traced here: 99.2 us
  blocking collectives  20.4 us (20%)
  starting transfers between devices  20.1 us (20%)
  between operations  18.9 us (19%)
  waiting for transfers between devices  12.5 us (13%)
  matrix products  11.8 us (12%)
  other arithmetic  9.16 us (9%)
  local copies, waits for them, and re-layouts  6.31 us (6%)
    all_to_all x1, blocking collectives, shards(): lax.all_to_all(result, 'eloc', split_axis=0, concat_axis=1, tiled=True)  20.4 us
    ppermute x1, waiting for transfers between devices, extended_2(): lax.ppermute(head, axis, [((i + 1) % count, i) for i in range(ends)])  11.2 us
    ppermute x1, starting transfers between devices, extended_2(): lax.ppermute(tail, axis, [(i, (i + 1) % count) for i in range(ends)])  9.65 us
    all_to_all x1, starting transfers between devices, shards(): lax.all_to_all(lesser[None].astype(jnp.bfloat16), 'eloc', split_axis=1, c...  8.36 us
    dot_general x1, matrix products, shards(): jnp.einsum('akij,akjl->ail', half_product, adjoint_form(blocks), preferre...  4.72 us
    add x2, other arithmetic, shards(): (occupancy[mode_index] + 1.0) * upper_part  4.51 us
    dot_general x6, matrix products, shards(): jnp.einsum('aij,eajl->eail', coupling_float[mode_index], widened_form(mix...  3.63 us
    dot_general x6, matrix products, shards(): jnp.einsum('eaij,ajl->eail', left, right_forms[mode_index], precision=lax...  3.4 us
  transfers between devices with their start and end apart: 3, of which 2 were waited for; matrix products, arithmetic and copies ran while one was open for 2% of the time, Pallas kernels for 0%

commit v1 on v0

v1 whole, which is shorter than its diff:
```python
import functools

import jax
import jax.numpy as jnp
from jax import lax
from jax.experimental import pallas as pl
from jax.experimental.pallas import tpu as pltpu
from jax.sharding import PartitionSpec as P

MESH = pl.DeviceIdType.MESH
RUN = 4


def signs(shape):
    half = shape[-1] // 2
    lane = lax.broadcasted_iota(jnp.int32, shape, len(shape) - 1)
    return jnp.where(lane < half, -1.0, 1.0).astype(jnp.float32)


def turned(block):
    wide = block.astype(jnp.float32)
    return pltpu.roll(wide, block.shape[-1] // 2, 1) * signs(block.shape)


def kernel(
    groups,
    near_ref,
    occ_ref,
    shift_ref,
    green_hbm,
    sigma_hbm,
    coup_ref,
    out_ref,
    green,
    sigma,
    wide,
    mine,
    ext,
    right,
    left,
    mid,
    res,
    in_sem,
    own_send,
    far_send,
    fwd_send,
    pair_send,
    ret_send,
    ext_recv,
    out_recv,
):
    atoms, orb, lanes = sigma.shape
    size = atoms
    modes = right.shape[0]
    chunk = 4
    run = min(RUN, size // 2)
    grp = lax.axis_index("egrp")
    loc = lax.axis_index("eloc")
    core = grp % 2
    partner = grp + 1 - 2 * core
    other = grp - 1 + 2 * core
    has_other = (other >= 0) & (other < groups)
    here = loc % run

    pieces = atoms // chunk
    loads = [
        pltpu.make_async_copy(
            green_hbm.at[0, pl.ds(p * chunk, chunk)],
            green.at[pl.ds(p * chunk, chunk)],
            in_sem.at[p],
        )
        for p in range(pieces)
    ]
    load_sigma = pltpu.make_async_copy(sigma_hbm.at[0], sigma, in_sem.at[pieces])
    load_sigma.start()
    for load in loads:
        load.start()

    barrier = pltpu.get_barrier_semaphore()

    def greet(i, carry):
        @pl.when(i != loc)
        def _():
            pl.semaphore_signal(
                barrier, inc=1, device_id=(grp, i), device_id_type=MESH
            )

        @pl.when(has_other)
        def _():
            pl.semaphore_signal(
                barrier, inc=1, device_id=(other, i), device_id_type=MESH
            )

        return carry

    lax.fori_loop(0, size, greet, 0)
    pl.semaphore_signal(
        barrier, inc=1, device_id=(partner, loc), device_id_type=MESH
    )

    load_sigma.wait()

    def widen(n, carry):
        block = sigma[n]
        wide[n, :orb] = block
        wide[n, orb:] = turned(block).astype(jnp.bfloat16)
        return carry

    lax.fori_loop(0, atoms, widen, 0, unroll=2)

    def lesser(a, carry):
        total = jnp.zeros((orb, lanes), jnp.float32)
        for k in range(3):
            n = a if k == 0 else near_ref[k - 1, a]
            block = green[a, k]
            half = jnp.dot(
                block, wide[n], preferred_element_type=jnp.float32
            ).astype(jnp.bfloat16)
            form = jnp.concatenate([block, turned(block).astype(jnp.bfloat16)], 0)
            total = total + lax.dot_general(
                half, form, (((1,), (1,)), ((), ())), preferred_element_type=jnp.float32
            )
        mine[a] = total.astype(jnp.bfloat16)
        return carry

    for p in range(pieces):
        loads[p].wait()
        lax.fori_loop(p * chunk, (p + 1) * chunk, lesser, 0, unroll=2)

    @pl.when(has_other)
    def _():
        pl.semaphore_wait(barrier, 2 * size)

    @pl.when(jnp.logical_not(has_other))
    def _():
        pl.semaphore_wait(barrier, size)

    far_base = 2 * size * (1 - core)
    pair_base = 2 * size * core

    def own_copy(a):
        return pltpu.make_async_remote_copy(
            src_ref=mine.at[a],
            dst_ref=ext.at[size + loc],
            send_sem=own_send.at[a],
            recv_sem=ext_recv.at[size + loc],
            device_id=(grp, a),
            device_id_type=MESH,
        )

    def far_copy(a):
        return pltpu.make_async_remote_copy(
            src_ref=mine.at[a],
            dst_ref=ext.at[far_base + loc],
            send_sem=far_send.at[a],
            recv_sem=ext_recv.at[far_base + loc],
            device_id=(other, a),
            device_id_type=MESH,
        )

    def forward_copy(j):
        return pltpu.make_async_remote_copy(
            src_ref=ext.at[size + j],
            dst_ref=ext.at[far_base + j],
            send_sem=fwd_send.at[j],
            recv_sem=ext_recv.at[far_base + j],
            device_id=(other, loc),
            device_id_type=MESH,
        )

    def pair_copy(j):
        return pltpu.make_async_remote_copy(
            src_ref=ext.at[size + j],
            dst_ref=ext.at[pair_base + j],
            send_sem=pair_send.at[j],
            recv_sem=ext_recv.at[pair_base + j],
            device_id=(partner, loc),
            device_id_type=MESH,
        )

    def straight(source, worker):
        rise = source % run - worker % run
        return (rise * (2 * core - 1) >= 0) & (source != worker)

    def arrived(slot):
        pltpu.make_async_remote_copy(
            src_ref=ext.at[slot],
            dst_ref=ext.at[slot],
            send_sem=own_send.at[0],
            recv_sem=ext_recv.at[slot],
            device_id=(partner, loc),
            device_id_type=MESH,
        ).wait_recv()

    def send(t, carry):
        a = (loc + t) % size

        @pl.when(has_other & straight(loc, a))
        def _():
            far_copy(a).start()

        own_copy(a).start()
        return carry

    ext[size + loc] = mine[loc]
    lax.fori_loop(1, size, send, 0)

    for m in range(modes):
        block = coup_ref[m, 0].astype(jnp.float32)
        adjoint = jnp.concatenate([block, turned(coup_ref[m, 0])], 0).T
        right[m, :lanes] = (adjoint * (occ_ref[m] + 1.0)).astype(jnp.bfloat16)
        right[m, lanes:] = (adjoint * occ_ref[m]).astype(jnp.bfloat16)
    low = lax.broadcasted_iota(jnp.int32, (orb, lanes), 1) < orb
    for m in range(0, modes, 2):
        one = coup_ref[m, 0].astype(jnp.float32)
        two = coup_ref[m + 1, 0].astype(jnp.float32)
        span = slice(m * orb, m * orb + lanes)
        left[:orb, span] = jnp.where(low, one, pltpu.roll(two, orb, 1)).astype(
            jnp.bfloat16
        )
        left[orb:, span] = jnp.where(low, pltpu.roll(one, orb, 1), two).astype(
            jnp.bfloat16
        )

    def relay(t, carry):
        j = (loc + size - t) % size

        @pl.when(t > 0)
        def _():
            arrived(size + j)

        @pl.when(has_other & jnp.logical_not(straight(j, loc)))
        def _():
            forward_copy(j).start()

        pair_copy(j).start()
        return carry

    lax.fori_loop(0, size, relay, 0)

    def halo(j, carry):
        arrived(pair_other + j)

        @pl.when(has_other)
        def _():
            arrived(far_other + j)

        return carry

    pair_other = 2 * size * (1 - core)
    far_other = 2 * size * core
    lax.fori_loop(0, size, halo, 0)

    @pl.when(jnp.logical_not(has_other))
    def _():
        ext[pl.ds(far_other, size)] = jnp.zeros((size, orb, lanes), ext.dtype)

    def ret_copy(i):
        return pltpu.make_async_remote_copy(
            src_ref=res.at[i],
            dst_ref=out_ref.at[0, loc],
            send_sem=ret_send.at[i],
            recv_sem=out_recv.at[loc],
            device_id=(grp, i),
            device_id_type=MESH,
        )

    def mix(q, carry):
        first = ((loc // run + q) % pieces) * chunk
        for m in range(modes):
            above = ext[pl.ds(size + first + shift_ref[m], chunk)]
            below = ext[pl.ds(size + first - shift_ref[m], chunk)]
            both = jnp.concatenate(
                [above.reshape(chunk * orb, lanes), below.reshape(chunk * orb, lanes)], 1
            )
            product = jnp.dot(both, right[m], preferred_element_type=jnp.float32)
            mid[:, m * orb : (m + 1) * orb] = product.astype(jnp.bfloat16).reshape(
                chunk, orb, lanes
            )
        for i in range(chunk):
            parts = jnp.dot(left[...], mid[i], preferred_element_type=jnp.float32)
            value = parts[:orb] + pltpu.roll(parts[orb:], orb, 1) * signs((orb, lanes))
            res[first + i] = value.astype(jnp.bfloat16)
        for i in range(chunk):

            @pl.when(first + i != loc)
            def _():
                ret_copy(first + i).start()

        return carry

    lax.fori_loop(0, pieces, mix, 0)
    out_ref[0, loc] = res[loc]

    def settle(i, carry):
        @pl.when(i != loc)
        def _():
            pltpu.make_async_remote_copy(
                src_ref=res.at[i],
                dst_ref=out_ref.at[0, i],
                send_sem=ret_send.at[i],
                recv_sem=out_recv.at[i],
                device_id=(grp, i),
                device_id_type=MESH,
            ).wait()
            own_copy(i).wait_send()

        @pl.when(has_other & straight(loc, i))
        def _():
            far_copy(i).wait_send()

        @pl.when(has_other & jnp.logical_not(straight(i, loc)))
        def _():
            forward_copy(i).wait_send()

        pair_copy(i).wait_send()
        return carry

    lax.fori_loop(0, size, settle, 0)


def solution(mesh):
    groups = mesh.shape["egrp"]

    def step(green_blocks, sigma_prev, neighbours, couplings, occupancy, shifts):
        _, atoms, hops, orb, lanes = green_blocks.shape
        modes = couplings.shape[0]
        size = atoms
        vmem = pl.BlockSpec(memory_space=pltpu.VMEM)
        smem = pl.BlockSpec(memory_space=pltpu.SMEM)
        hbm = pl.BlockSpec(memory_space=pl.ANY)
        half = jnp.bfloat16
        return pl.pallas_call(
            functools.partial(kernel, groups),
            out_shape=jax.ShapeDtypeStruct((1, atoms, orb, lanes), half),
            in_specs=[smem, smem, smem, hbm, hbm, vmem],
            out_specs=vmem,
            scratch_shapes=[
                pltpu.VMEM((atoms, hops, orb, lanes), half),
                pltpu.VMEM((atoms, orb, lanes), half),
                pltpu.VMEM((atoms, lanes, lanes), half),
                pltpu.VMEM((atoms, orb, lanes), half),
                pltpu.VMEM((3 * size, orb, lanes), half),
                pltpu.VMEM((modes, 2 * lanes, lanes), half),
                pltpu.VMEM((lanes, modes * orb), half),
                pltpu.VMEM((4, modes * orb, lanes), half),
                pltpu.VMEM((size, orb, lanes), half),
                pltpu.SemaphoreType.DMA((atoms // 4 + 1,)),
                pltpu.SemaphoreType.DMA((size,)),
                pltpu.SemaphoreType.DMA((size,)),
                pltpu.SemaphoreType.DMA((size,)),
                pltpu.SemaphoreType.DMA((size,)),
                pltpu.SemaphoreType.DMA((size,)),
                pltpu.SemaphoreType.DMA((3 * size,)),
                pltpu.SemaphoreType.DMA((size,)),
            ],
            compiler_params=pltpu.CompilerParams(
                collective_id=0, has_side_effects=True
            ),
        )(neighbours.T, occupancy, shifts, green_blocks, sigma_prev, couplings)

    return jax.shard_map(
        step,
        mesh=mesh,
        in_specs=(
            P(("egrp", "eloc"), None, None, None, None),
            P(("egrp", "eloc"), None, None, None),
            P(),
            P(None, "eloc", None, None),
            P(),
            P(),
        ),
        out_specs=P(("egrp", "eloc"), None, None, None),
        check_vma=False,
    )
```

time: 99.8 us -> 45.1 us (0.45)
  the two profiles are of different devices: /device:TPU:5 before, /device:TPU:6 now
where the time goes in v1:
time: 45.1 us; the launch traced here: 44.9 us
  Pallas kernels  43.3 us (96%)
  local copies, waits for them, and re-layouts  1.67 us (4%)
    pallas_call x1, Pallas kernels, step(): pl.pallas_call(functools.partial(kernel, groups), out_shape=jax.ShapeDtyp...  43.3 us
    unnamed x1, local copies, waits for them, and re-layouts  1.67 us

profile of v1, /device:TPU:6, one launch (start us, length us, event | category | flops | bytes accessed | tf_op | source)
XLA Modules:
  0.0 44.9 jit_solution(5496031884851146491)
XLA Ops:
  0.0 43.3 %shard_map.64 = bf16[1,16,64,128]{3,2,1,0:T(8,128)(2,1)} custom-call(s32[2,16]{1,0:T(2,128)} %bitcast.1, f32[6]{0:T(128)} %occ_ref.1, s32[6]{0:T(128)} %shift_ref.1, bf16[1,16,3,64,128]{4,3,2,1,0:T(8,128)(2,1)} %green_hbm.1, bf16[1,16,64,128]{3,2,1,0:T(8,128)(2,1)} %sigma_hbm.1, bf16[6,1,64,128]{3,2,1,0:T(8,128)(2,1)} %coup_ref.1), custom_call_target="tpu_custom_call" | custom-call | tf_op jit(solution)/shard_map/pallas_call | solution.py:333
  43.3 1.7 %copy.8 = bf16[1,16,64,128]{3,2,1,0:T(8,128)(2,1)} copy(bf16[1,16,64,128]{3,2,1,0:T(8,128)(2,1)} %shard_map.64) | data formatting | bytes 524288

commit v2 on v1

--- a/solution.py
+++ b/solution.py
@@ -24,15 +24,19 @@
 
 def kernel(
     groups,
+    near_hbm,
+    occ_hbm,
+    shift_hbm,
+    green_hbm,
+    sigma_hbm,
+    coup_hbm,
+    out_ref,
     near_ref,
     occ_ref,
     shift_ref,
-    green_hbm,
-    sigma_hbm,
-    coup_ref,
-    out_ref,
     green,
     sigma,
+    coup_ref,
     wide,
     mine,
     ext,
@@ -53,6 +57,7 @@
     size = atoms
     modes = right.shape[0]
     chunk = 4
+    lag = min(4, size // 2)
     run = min(RUN, size // 2)
     grp = lax.axis_index("egrp")
     loc = lax.axis_index("eloc")
@@ -63,18 +68,31 @@
     here = loc % run
 
     pieces = atoms // chunk
-    loads = [
-        pltpu.make_async_copy(
-            green_hbm.at[0, pl.ds(p * chunk, chunk)],
-            green.at[pl.ds(p * chunk, chunk)],
-            in_sem.at[p],
-        )
-        for p in range(pieces)
-    ]
-    load_sigma = pltpu.make_async_copy(sigma_hbm.at[0], sigma, in_sem.at[pieces])
+
+    def turn(t):
+        return (loc + t) % size
+
+    def load_green(t):
+        return pltpu.make_async_copy(
+            green_hbm.at[0, turn(t)], green.at[turn(t)], in_sem.at[t - 1]
+        )
+
+    load_near = pltpu.make_async_copy(near_hbm, near_ref, in_sem.at[atoms])
+    load_sigma = pltpu.make_async_copy(sigma_hbm.at[0], sigma, in_sem.at[atoms + 1])
+    load_occ = pltpu.make_async_copy(occ_hbm, occ_ref, in_sem.at[atoms + 2])
+    load_shift = pltpu.make_async_copy(shift_hbm, shift_ref, in_sem.at[atoms + 3])
+    load_coup = pltpu.make_async_copy(coup_hbm, coup_ref, in_sem.at[atoms + 4])
     load_sigma.start()
-    for load in loads:
-        load.start()
+    load_near.start()
+
+    def fetch(t, carry):
+        load_green(t).start()
+        return carry
+
+    lax.fori_loop(1, size + 1, fetch, 0)
+    load_coup.start()
+    load_occ.start()
+    load_shift.start()
 
     barrier = pltpu.get_barrier_semaphore()
 
@@ -98,6 +116,7 @@
         barrier, inc=1, device_id=(partner, loc), device_id_type=MESH
     )
 
+    load_near.wait()
     load_sigma.wait()
 
     def widen(n, carry):
@@ -108,7 +127,9 @@
 
     lax.fori_loop(0, atoms, widen, 0, unroll=2)
 
-    def lesser(a, carry):
+    def lesser(t):
+        load_green(t).wait()
+        a = turn(t)
         total = jnp.zeros((orb, lanes), jnp.float32)
         for k in range(3):
             n = a if k == 0 else near_ref[k - 1, a]
@@ -121,11 +142,13 @@
                 half, form, (((1,), (1,)), ((), ())), preferred_element_type=jnp.float32
             )
         mine[a] = total.astype(jnp.bfloat16)
-        return carry
-
-    for p in range(pieces):
-        loads[p].wait()
-        lax.fori_loop(p * chunk, (p + 1) * chunk, lesser, 0, unroll=2)
+
+    def first(t, carry):
+        lesser(2 * t + 1)
+        lesser(2 * t + 2)
+        return carry
+
+    lax.fori_loop(0, lag // 2, first, 0)
 
     @pl.when(has_other)
     def _():
@@ -180,7 +203,7 @@
 
     def straight(source, worker):
         rise = source % run - worker % run
-        return (rise * (2 * core - 1) >= 0) & (source != worker)
+        return rise * (2 * core - 1) > 0
 
     def arrived(slot):
         pltpu.make_async_remote_copy(
@@ -192,19 +215,49 @@
             device_id_type=MESH,
         ).wait_recv()
 
-    def send(t, carry):
-        a = (loc + t) % size
+    def send(t):
+        a = turn(t)
 
         @pl.when(has_other & straight(loc, a))
         def _():
             far_copy(a).start()
 
         own_copy(a).start()
-        return carry
-
+
+    def later(t, carry):
+        send(2 * t + 1 - lag)
+        send(2 * t + 2 - lag)
+        lesser(2 * t + 1)
+        lesser(2 * t + 2)
+        return carry
+
+    def last(t, carry):
+        send(t)
+        return carry
+
+    lax.fori_loop(lag // 2, size // 2, later, 0)
+    lax.fori_loop(size - lag + 1, size, last, 0)
     ext[size + loc] = mine[loc]
-    lax.fori_loop(1, size, send, 0)
-
+
+    def relay(t, carry):
+        j = (loc + size - t) % size
+
+        @pl.when(t > 0)
+        def _():
+            arrived(size + j)
+
+        @pl.when(has_other & jnp.logical_not(straight(j, loc)))
+        def _():
+            forward_copy(j).start()
+
+        pair_copy(j).start()
+        return carry
+
+    lax.fori_loop(0, size, relay, 0)
+
+    load_coup.wait()
+    load_occ.wait()
+    load_shift.wait()
     for m in range(modes):
         block = coup_ref[m, 0].astype(jnp.float32)
         adjoint = jnp.concatenate([block, turned(coup_ref[m, 0])], 0).T
@@ -221,22 +274,6 @@
         left[orb:, span] = jnp.where(low, pltpu.roll(one, orb, 1), two).astype(
             jnp.bfloat16
         )
-
-    def relay(t, carry):
-        j = (loc + size - t) % size
-
-        @pl.when(t > 0)
-        def _():
-            arrived(size + j)
-
-        @pl.when(has_other & jnp.logical_not(straight(j, loc)))
-        def _():
-            forward_copy(j).start()
-
-        pair_copy(j).start()
-        return carry
-
-    lax.fori_loop(0, size, relay, 0)
 
     def halo(j, carry):
         arrived(pair_other + j)
@@ -327,17 +364,20 @@
         modes = couplings.shape[0]
         size = atoms
         vmem = pl.BlockSpec(memory_space=pltpu.VMEM)
-        smem = pl.BlockSpec(memory_space=pltpu.SMEM)
         hbm = pl.BlockSpec(memory_space=pl.ANY)
         half = jnp.bfloat16
         return pl.pallas_call(
             functools.partial(kernel, groups),
-            out_shape=jax.ShapeDtypeStruct((1, atoms, orb, lanes), half),
-            in_specs=[smem, smem, smem, hbm, hbm, vmem],
+            out_shape=pltpu.VMEM((1, atoms, orb, lanes), half),
+            in_specs=[hbm] * 6,
             out_specs=vmem,
             scratch_shapes=[
+                pltpu.SMEM(neighbours.shape[::-1], jnp.int32),
+                pltpu.SMEM((modes,), jnp.float32),
+                pltpu.SMEM((modes,), jnp.int32),
                 pltpu.VMEM((atoms, hops, orb, lanes), half),
                 pltpu.VMEM((atoms, orb, lanes), half),
+                pltpu.VMEM(couplings.shape, half),
                 pltpu.VMEM((atoms, lanes, lanes), half),
                 pltpu.VMEM((atoms, orb, lanes), half),
                 pltpu.VMEM((3 * size, orb, lanes), half),
@@ -345,7 +385,7 @@
                 pltpu.VMEM((lanes, modes * orb), half),
                 pltpu.VMEM((4, modes * orb, lanes), half),
                 pltpu.VMEM((size, orb, lanes), half),
-                pltpu.SemaphoreType.DMA((atoms // 4 + 1,)),
+                pltpu.SemaphoreType.DMA((atoms + 5,)),
                 pltpu.SemaphoreType.DMA((size,)),
                 pltpu.SemaphoreType.DMA((size,)),
                 pltpu.SemaphoreType.DMA((size,)),

time: 45.1 us -> 41.3 us (0.916)
  the two profiles are of different devices: /device:TPU:6 before, /device:TPU:2 now
where the time goes in v2:
time: 41.3 us; the launch traced here: 41.2 us
  Pallas kernels  40.4 us (98%)
  local copies, waits for them, and re-layouts  0.71 us (2%)
    pallas_call x1, Pallas kernels, step(): pl.pallas_call(functools.partial(kernel, groups), out_shape=pltpu.VMEM((1...  40.4 us

profile of v2, /device:TPU:2, one launch (start us, length us, event | category | flops | bytes accessed | tf_op | source)
XLA Modules:
  0.0 41.2 jit_solution(14280180936273977421)
XLA Ops:
  0.0 40.4 %shard_map.64 = bf16[1,16,64,128]{3,2,1,0:T(8,128)(2,1)S(1)} custom-call(s32[2,16]{1,0:T(2,128)} %bitcast.1, f32[6]{0:T(128)} %occ_hbm.1, s32[6]{0:T(128)} %shift_hbm.1, bf16[1,16,3,64,128]{4,3,2,1,0:T(8,128)(2,1)} %green_hbm.1, bf16[1,16,64,128]{3,2,1,0:T(8,128)(2,1)} %sigma_hbm.1, bf16[6,1,64,128]{3,2,1,0:T(8,128)(2,1)} %coup_hbm.1), custom_call_target="tpu_custom_call" | custom-call | tf_op jit(solution)/shard_map/pallas_call | solution.py:369
  40.5 0.7 %copy.8 = bf16[1,16,64,128]{3,2,1,0:T(8,128)(2,1)} copy(bf16[1,16,64,128]{3,2,1,0:T(8,128)(2,1)S(1)} %shard_map.64) | data formatting | bytes 524288

commit v3 on v2

--- a/solution.py
+++ b/solution.py
@@ -39,11 +39,14 @@
     coup_ref,
     wide,
     mine,
+    own,
     ext,
     right,
     left,
     mid,
     res,
+    given,
+    part,
     in_sem,
     own_send,
     far_send,
@@ -52,6 +55,10 @@
     ret_send,
     ext_recv,
     out_recv,
+    give_send,
+    part_recv,
+    far_sem,
+    all_sem,
 ):
     atoms, orb, lanes = sigma.shape
     size = atoms
@@ -94,6 +101,22 @@
     load_occ.start()
     load_shift.start()
 
+    def straight(source, worker):
+        rise = source % run - worker % run
+        return rise * (2 * core - 1) > 0
+
+    def exports(worker):
+        return worker % run // (run // 2) != core
+
+    exporter = has_other & exports(loc)
+    importer = has_other & jnp.logical_not(exports(loc))
+
+    def reaches(i):
+        return straight(loc, i) | (i == loc)
+
+    hi = (grp // 2) % 4
+    lead = jnp.where(core == 1, jnp.where(hi == 3, 0, 1), jnp.where(hi == 0, 1, 0))
+    nearer = (core * here + (1 - core) * (run - 1 - here)) * (size // run)
     barrier = pltpu.get_barrier_semaphore()
 
     def greet(i, carry):
@@ -103,7 +126,7 @@
                 barrier, inc=1, device_id=(grp, i), device_id_type=MESH
             )
 
-        @pl.when(has_other)
+        @pl.when(has_other & (lead == 1) & reaches(i))
         def _():
             pl.semaphore_signal(
                 barrier, inc=1, device_id=(other, i), device_id_type=MESH
@@ -116,6 +139,8 @@
         barrier, inc=1, device_id=(partner, loc), device_id_type=MESH
     )
 
+    own[pl.ds(0, size)] = jnp.zeros((size, orb, lanes), own.dtype)
+    own[pl.ds(2 * size, size)] = jnp.zeros((size, orb, lanes), own.dtype)
     load_near.wait()
     load_sigma.wait()
 
@@ -150,11 +175,22 @@
 
     lax.fori_loop(0, lag // 2, first, 0)
 
-    @pl.when(has_other)
+    @pl.when(has_other & (lead == 0))
     def _():
-        pl.semaphore_wait(barrier, 2 * size)
-
-    @pl.when(jnp.logical_not(has_other))
+        pl.semaphore_wait(barrier, size + 1 + nearer)
+
+        def answer(i, carry):
+            @pl.when(reaches(i))
+            def _():
+                pl.semaphore_signal(
+                    far_sem, inc=1, device_id=(other, i), device_id_type=MESH
+                )
+
+            return carry
+
+        lax.fori_loop(0, size, answer, 0)
+
+    @pl.when(jnp.logical_not(has_other & (lead == 0)))
     def _():
         pl.semaphore_wait(barrier, size)
 
@@ -164,7 +200,7 @@
     def own_copy(a):
         return pltpu.make_async_remote_copy(
             src_ref=mine.at[a],
-            dst_ref=ext.at[size + loc],
+            dst_ref=own.at[size + loc],
             send_sem=own_send.at[a],
             recv_sem=ext_recv.at[size + loc],
             device_id=(grp, a),
@@ -183,7 +219,7 @@
 
     def forward_copy(j):
         return pltpu.make_async_remote_copy(
-            src_ref=ext.at[size + j],
+            src_ref=own.at[size + j],
             dst_ref=ext.at[far_base + j],
             send_sem=fwd_send.at[j],
             recv_sem=ext_recv.at[far_base + j],
@@ -193,17 +229,13 @@
 
     def pair_copy(j):
         return pltpu.make_async_remote_copy(
-            src_ref=ext.at[size + j],
+            src_ref=own.at[size + j],
             dst_ref=ext.at[pair_base + j],
             send_sem=pair_send.at[j],
             recv_sem=ext_recv.at[pair_base + j],
             device_id=(partner, loc),
             device_id_type=MESH,
         )
-
-    def straight(source, worker):
-        rise = source % run - worker % run
-        return rise * (2 * core - 1) > 0
 
     def arrived(slot):
         pltpu.make_async_remote_copy(
@@ -218,7 +250,7 @@
     def send(t):
         a = turn(t)
 
-        @pl.when(has_other & straight(loc, a))
+        @pl.when(has_other & (lead == 0) & straight(loc, a) & exports(a))
         def _():
             far_copy(a).start()
 
@@ -237,23 +269,58 @@
 
     lax.fori_loop(lag // 2, size // 2, later, 0)
     lax.fori_loop(size - lag + 1, size, last, 0)
-    ext[size + loc] = mine[loc]
-
-    def relay(t, carry):
-        j = (loc + size - t) % size
-
+    own[size + loc] = mine[loc]
+
+    def source(t):
+        return (loc + size - t) % size
+
+    def forward(t):
+        @pl.when(exporter & jnp.logical_not(straight(source(t), loc)))
+        def _():
+            forward_copy(source(t)).start()
+
+    def early(t, carry):
         @pl.when(t > 0)
         def _():
-            arrived(size + j)
-
-        @pl.when(has_other & jnp.logical_not(straight(j, loc)))
-        def _():
-            forward_copy(j).start()
-
-        pair_copy(j).start()
-        return carry
-
-    lax.fori_loop(0, size, relay, 0)
+            arrived(size + source(t))
+
+        @pl.when(lead == 0)
+        def _():
+            forward(t)
+
+        pair_copy(source(t)).start()
+        return carry
+
+    def late(t, carry):
+        arrived(size + source(t))
+        forward(t)
+        pair_copy(source(t)).start()
+        return carry
+
+    lax.fori_loop(0, size // 2, early, 0)
+
+    @pl.when(has_other & (lead == 1))
+    def _():
+        pl.semaphore_wait(far_sem, 1 + nearer)
+        pl.semaphore_signal(
+            all_sem, inc=1, device_id=(other, loc), device_id_type=MESH
+        )
+
+        def direct(t, carry):
+            @pl.when(straight(loc, turn(t)) & exports(turn(t)))
+            def _():
+                far_copy(turn(t)).start()
+
+            return carry
+
+        def delayed(t, carry):
+            forward(t)
+            return carry
+
+        lax.fori_loop(1, size, direct, 0)
+        lax.fori_loop(0, size // 2, delayed, 0)
+
+    lax.fori_loop(size // 2, size, late, 0)
 
     load_coup.wait()
     load_occ.wait()
@@ -275,10 +342,54 @@
             jnp.bfloat16
         )
 
+    ext[pl.ds(size, size)] = own[pl.ds(size, size)]
+
+    @pl.when(has_other & (lead == 0))
+    def _():
+        pl.semaphore_wait(all_sem, 1)
+
+    def give_copy(i):
+        return pltpu.make_async_remote_copy(
+            src_ref=given.at[i],
+            dst_ref=part.at[loc],
+            send_sem=give_send.at[i],
+            recv_sem=part_recv.at[loc],
+            device_id=(other, i),
+            device_id_type=MESH,
+        )
+
+    def finish(m_blocks, target, first):
+        for i in range(chunk):
+            parts = jnp.dot(left[...], m_blocks[i], preferred_element_type=jnp.float32)
+            value = parts[:orb] + pltpu.roll(parts[orb:], orb, 1) * signs((orb, lanes))
+            target[first + i] = value.astype(jnp.bfloat16)
+
+    @pl.when(importer)
+    def _():
+        def give(q, carry):
+            first = ((loc // run + q) % pieces) * chunk
+            for m in range(modes):
+                start = first + shift_ref[m] + core * (2 * size - 2 * shift_ref[m])
+                block = own[pl.ds(start, chunk)].reshape(chunk * orb, lanes)
+                product = jnp.dot(
+                    block,
+                    right[m, pl.ds(core * lanes, lanes)],
+                    preferred_element_type=jnp.float32,
+                )
+                mid[:, m * orb : (m + 1) * orb] = product.astype(
+                    jnp.bfloat16
+                ).reshape(chunk, orb, lanes)
+            finish(mid, given, first)
+            for i in range(chunk):
+                give_copy(first + i).start()
+            return carry
+
+        lax.fori_loop(0, pieces, give, 0)
+
     def halo(j, carry):
         arrived(pair_other + j)
 
-        @pl.when(has_other)
+        @pl.when(importer)
         def _():
             arrived(far_other + j)
 
@@ -288,7 +399,7 @@
     far_other = 2 * size * core
     lax.fori_loop(0, size, halo, 0)
 
-    @pl.when(jnp.logical_not(has_other))
+    @pl.when(jnp.logical_not(importer))
     def _():
         ext[pl.ds(far_other, size)] = jnp.zeros((size, orb, lanes), ext.dtype)
 
@@ -314,10 +425,7 @@
             mid[:, m * orb : (m + 1) * orb] = product.astype(jnp.bfloat16).reshape(
                 chunk, orb, lanes
             )
-        for i in range(chunk):
-            parts = jnp.dot(left[...], mid[i], preferred_element_type=jnp.float32)
-            value = parts[:orb] + pltpu.roll(parts[orb:], orb, 1) * signs((orb, lanes))
-            res[first + i] = value.astype(jnp.bfloat16)
+        finish(mid, res, first)
         for i in range(chunk):
 
             @pl.when(first + i != loc)
@@ -342,13 +450,30 @@
             ).wait()
             own_copy(i).wait_send()
 
-        @pl.when(has_other & straight(loc, i))
-        def _():
-            far_copy(i).wait_send()
-
-        @pl.when(has_other & jnp.logical_not(straight(i, loc)))
+        @pl.when(has_other & exports(i))
+        def _():
+            pltpu.make_async_remote_copy(
+                src_ref=given.at[i],
+                dst_ref=part.at[i],
+                send_sem=give_send.at[i],
+                recv_sem=part_recv.at[i],
+                device_id=(other, i),
+                device_id_type=MESH,
+            ).wait_recv()
+            total = out_ref[0, i].astype(jnp.float32) + part[i].astype(jnp.float32)
+            out_ref[0, i] = total.astype(jnp.bfloat16)
+
+            @pl.when(straight(loc, i))
+            def _():
+                far_copy(i).wait_send()
+
+        @pl.when(exporter & jnp.logical_not(straight(i, loc)))
         def _():
             forward_copy(i).wait_send()
+
+        @pl.when(importer)
+        def _():
+            give_copy(i).wait_send()
 
         pair_copy(i).wait_send()
         return carry
@@ -381,10 +506,13 @@
                 pltpu.VMEM((atoms, lanes, lanes), half),
                 pltpu.VMEM((atoms, orb, lanes), half),
                 pltpu.VMEM((3 * size, orb, lanes), half),
+                pltpu.VMEM((3 * size, orb, lanes), half),
                 pltpu.VMEM((modes, 2 * lanes, lanes), half),
                 pltpu.VMEM((lanes, modes * orb), half),
                 pltpu.VMEM((4, modes * orb, lanes), half),
                 pltpu.VMEM((size, orb, lanes), half),
+                pltpu.VMEM((size, orb, lanes), half),
+                pltpu.VMEM((size, orb, lanes), half),
                 pltpu.SemaphoreType.DMA((atoms + 5,)),
                 pltpu.SemaphoreType.DMA((size,)),
                 pltpu.SemaphoreType.DMA((size,)),
@@ -393,6 +521,10 @@
                 pltpu.SemaphoreType.DMA((size,)),
                 pltpu.SemaphoreType.DMA((3 * size,)),
                 pltpu.SemaphoreType.DMA((size,)),
+                pltpu.SemaphoreType.DMA((size,)),
+                pltpu.SemaphoreType.DMA((size,)),
+                pltpu.SemaphoreType.REGULAR,
+                pltpu.SemaphoreType.REGULAR,
             ],
             compiler_params=pltpu.CompilerParams(
                 collective_id=0, has_side_effects=True

time: 41.3 us -> 36.9 us (0.89)
  the two profiles are of different devices: /device:TPU:2 before, /device:TPU:1 now
where the time goes in v3:
time: 36.9 us; the launch traced here: 36.8 us
  Pallas kernels  36.1 us (98%)
  local copies, waits for them, and re-layouts  0.71 us (2%)
    pallas_call x1, Pallas kernels, step(): pl.pallas_call(functools.partial(kernel, groups), out_shape=pltpu.VMEM((1...  36.1 us

profile of v3, /device:TPU:1, one launch (start us, length us, event | category | flops | bytes accessed | tf_op | source)
XLA Modules:
  0.0 36.8 jit_solution(5395359273621155879)
XLA Ops:
  0.0 36.1 %shard_map.64 = bf16[1,16,64,128]{3,2,1,0:T(8,128)(2,1)S(1)} custom-call(s32[2,16]{1,0:T(2,128)} %bitcast.1, f32[6]{0:T(128)} %occ_hbm.1, s32[6]{0:T(128)} %shift_hbm.1, bf16[1,16,3,64,128]{4,3,2,1,0:T(8,128)(2,1)} %green_hbm.1, bf16[1,16,64,128]{3,2,1,0:T(8,128)(2,1)} %sigma_hbm.1, bf16[6,1,64,128]{3,2,1,0:T(8,128)(2,1)} %coup_hbm.1), custom_call_target="tpu_custom_call" | custom-call | tf_op jit(solution)/shard_map/pallas_call | solution.py:494
  36.1 0.7 %copy.8 = bf16[1,16,64,128]{3,2,1,0:T(8,128)(2,1)} copy(bf16[1,16,64,128]{3,2,1,0:T(8,128)(2,1)S(1)} %shard_map.64) | data formatting | bytes 524288

commit v4 on v3

--- a/solution.py
+++ b/solution.py
@@ -64,7 +64,8 @@
     size = atoms
     modes = right.shape[0]
     chunk = 4
-    lag = min(4, size // 2)
+    batch = min(4, size // 2)
+    lag = batch
     run = min(RUN, size // 2)
     grp = lax.axis_index("egrp")
     loc = lax.axis_index("eloc")
@@ -152,175 +153,40 @@
 
     lax.fori_loop(0, atoms, widen, 0, unroll=2)
 
-    def lesser(t):
-        load_green(t).wait()
-        a = turn(t)
-        total = jnp.zeros((orb, lanes), jnp.float32)
-        for k in range(3):
-            n = a if k == 0 else near_ref[k - 1, a]
-            block = green[a, k]
-            half = jnp.dot(
-                block, wide[n], preferred_element_type=jnp.float32
+    def lesser(start):
+        for t in range(batch):
+            load_green(start + t).wait()
+        halves = []
+        for t in range(batch):
+            a = turn(start + t)
+            row = []
+            for k in range(3):
+                n = a if k == 0 else near_ref[k - 1, a]
+                row.append(
+                    jnp.dot(
+                        green[a, k], wide[n], preferred_element_type=jnp.float32
+                    ).astype(jnp.bfloat16)
+                )
+            halves.append(jnp.concatenate(row, 1))
+        for t in range(batch):
+            a = turn(start + t)
+            upper = jnp.concatenate([green[a, k] for k in range(3)], 1)
+            lower = jnp.concatenate(
+                [turned(green[a, k]).astype(jnp.bfloat16) for k in range(3)], 1
+            )
+            form = jnp.concatenate([upper, lower], 0)
+            mine[a] = lax.dot_general(
+                halves[t],
+                form,
+                (((1,), (1,)), ((), ())),
+                preferred_element_type=jnp.float32,
             ).astype(jnp.bfloat16)
-            form = jnp.concatenate([block, turned(block).astype(jnp.bfloat16)], 0)
-            total = total + lax.dot_general(
-                half, form, (((1,), (1,)), ((), ())), preferred_element_type=jnp.float32
-            )
-        mine[a] = total.astype(jnp.bfloat16)
 
     def first(t, carry):
-        lesser(2 * t + 1)
-        lesser(2 * t + 2)
-        return carry
-
-    lax.fori_loop(0, lag // 2, first, 0)
-
-    @pl.when(has_other & (lead == 0))
-    def _():
-        pl.semaphore_wait(barrier, size + 1 + nearer)
-
-        def answer(i, carry):
-            @pl.when(reaches(i))
-            def _():
-                pl.semaphore_signal(
-                    far_sem, inc=1, device_id=(other, i), device_id_type=MESH
-                )
-
-            return carry
-
-        lax.fori_loop(0, size, answer, 0)
-
-    @pl.when(jnp.logical_not(has_other & (lead == 0)))
-    def _():
-        pl.semaphore_wait(barrier, size)
-
-    far_base = 2 * size * (1 - core)
-    pair_base = 2 * size * core
-
-    def own_copy(a):
-        return pltpu.make_async_remote_copy(
-            src_ref=mine.at[a],
-            dst_ref=own.at[size + loc],
-            send_sem=own_send.at[a],
-            recv_sem=ext_recv.at[size + loc],
-            device_id=(grp, a),
-            device_id_type=MESH,
-        )
-
-    def far_copy(a):
-        return pltpu.make_async_remote_copy(
-            src_ref=mine.at[a],
-            dst_ref=ext.at[far_base + loc],
-            send_sem=far_send.at[a],
-            recv_sem=ext_recv.at[far_base + loc],
-            device_id=(other, a),
-            device_id_type=MESH,
-        )
-
-    def forward_copy(j):
-        return pltpu.make_async_remote_copy(
-            src_ref=own.at[size + j],
-            dst_ref=ext.at[far_base + j],
-            send_sem=fwd_send.at[j],
-            recv_sem=ext_recv.at[far_base + j],
-            device_id=(other, loc),
-            device_id_type=MESH,
-        )
-
-    def pair_copy(j):
-        return pltpu.make_async_remote_copy(
-            src_ref=own.at[size + j],
-            dst_ref=ext.at[pair_base + j],
-            send_sem=pair_send.at[j],
-            recv_sem=ext_recv.at[pair_base + j],
-            device_id=(partner, loc),
-            device_id_type=MESH,
-        )
-
-    def arrived(slot):
-        pltpu.make_async_remote_copy(
-            src_ref=ext.at[slot],
-            dst_ref=ext.at[slot],
-            send_sem=own_send.at[0],
-            recv_sem=ext_recv.at[slot],
-            device_id=(partner, loc),
-            device_id_type=MESH,
-        ).wait_recv()
-
-    def send(t):
-        a = turn(t)
-
-        @pl.when(has_other & (lead == 0) & straight(loc, a) & exports(a))
-        def _():
-            far_copy(a).start()
-
-        own_copy(a).start()
-
-    def later(t, carry):
-        send(2 * t + 1 - lag)
-        send(2 * t + 2 - lag)
-        lesser(2 * t + 1)
-        lesser(2 * t + 2)
-        return carry
-
-    def last(t, carry):
-        send(t)
-        return carry
-
-    lax.fori_loop(lag // 2, size // 2, later, 0)
-    lax.fori_loop(size - lag + 1, size, last, 0)
-    own[size + loc] = mine[loc]
-
-    def source(t):
-        return (loc + size - t) % size
-
-    def forward(t):
-        @pl.when(exporter & jnp.logical_not(straight(source(t), loc)))
-        def _():
-            forward_copy(source(t)).start()
-
-    def early(t, carry):
-        @pl.when(t > 0)
-        def _():
-            arrived(size + source(t))
-
-        @pl.when(lead == 0)
-        def _():
-            forward(t)
-
-        pair_copy(source(t)).start()
-        return carry
-
-    def late(t, carry):
-        arrived(size + source(t))
-        forward(t)
-        pair_copy(source(t)).start()
-        return carry
-
-    lax.fori_loop(0, size // 2, early, 0)
-
-    @pl.when(has_other & (lead == 1))
-    def _():
-        pl.semaphore_wait(far_sem, 1 + nearer)
-        pl.semaphore_signal(
-            all_sem, inc=1, device_id=(other, loc), device_id_type=MESH
-        )
-
-        def direct(t, carry):
-            @pl.when(straight(loc, turn(t)) & exports(turn(t)))
-            def _():
-                far_copy(turn(t)).start()
-
-            return carry
-
-        def delayed(t, carry):
-            forward(t)
-            return carry
-
-        lax.fori_loop(1, size, direct, 0)
-        lax.fori_loop(0, size // 2, delayed, 0)
-
-    lax.fori_loop(size // 2, size, late, 0)
+        lesser(batch * t + 1)
+        return carry
+
+    lax.fori_loop(0, lag // batch, first, 0)
 
     load_coup.wait()
     load_occ.wait()
@@ -341,6 +207,152 @@
         left[orb:, span] = jnp.where(low, pltpu.roll(one, orb, 1), two).astype(
             jnp.bfloat16
         )
+
+    @pl.when(has_other & (lead == 0))
+    def _():
+        pl.semaphore_wait(barrier, size + 1 + nearer)
+
+        def answer(i, carry):
+            @pl.when(reaches(i))
+            def _():
+                pl.semaphore_signal(
+                    far_sem, inc=1, device_id=(other, i), device_id_type=MESH
+                )
+
+            return carry
+
+        lax.fori_loop(0, size, answer, 0)
+
+    @pl.when(jnp.logical_not(has_other & (lead == 0)))
+    def _():
+        pl.semaphore_wait(barrier, size)
+
+    far_base = 2 * size * (1 - core)
+    pair_base = 2 * size * core
+
+    def own_copy(a):
+        return pltpu.make_async_remote_copy(
+            src_ref=mine.at[a],
+            dst_ref=own.at[size + loc],
+            send_sem=own_send.at[a],
+            recv_sem=ext_recv.at[size + loc],
+            device_id=(grp, a),
+            device_id_type=MESH,
+        )
+
+    def far_copy(a):
+        return pltpu.make_async_remote_copy(
+            src_ref=mine.at[a],
+            dst_ref=ext.at[far_base + loc],
+            send_sem=far_send.at[a],
+            recv_sem=ext_recv.at[far_base + loc],
+            device_id=(other, a),
+            device_id_type=MESH,
+        )
+
+    def forward_copy(j):
+        return pltpu.make_async_remote_copy(
+            src_ref=own.at[size + j],
+            dst_ref=ext.at[far_base + j],
+            send_sem=fwd_send.at[j],
+            recv_sem=ext_recv.at[far_base + j],
+            device_id=(other, loc),
+            device_id_type=MESH,
+        )
+
+    def pair_copy(j):
+        return pltpu.make_async_remote_copy(
+            src_ref=own.at[size + j],
+            dst_ref=ext.at[pair_base + j],
+            send_sem=pair_send.at[j],
+            recv_sem=ext_recv.at[pair_base + j],
+            device_id=(partner, loc),
+            device_id_type=MESH,
+        )
+
+    def arrived(slot):
+        pltpu.make_async_remote_copy(
+            src_ref=ext.at[slot],
+            dst_ref=ext.at[slot],
+            send_sem=own_send.at[0],
+            recv_sem=ext_recv.at[slot],
+            device_id=(partner, loc),
+            device_id_type=MESH,
+        ).wait_recv()
+
+    def send(t):
+        a = turn(t)
+
+        own_copy(a).start()
+
+    def later(t, carry):
+        for i in range(batch):
+            send(batch * t + 1 - lag + i)
+        lesser(batch * t + 1)
+        return carry
+
+    def last(t, carry):
+        send(t)
+        return carry
+
+    lax.fori_loop(lag // batch, size // batch, later, 0)
+    lax.fori_loop(size - lag + 1, size, last, 0)
+    own[size + loc] = mine[loc]
+
+    def direct(t, carry):
+        @pl.when(straight(loc, turn(t)) & exports(turn(t)))
+        def _():
+            far_copy(turn(t)).start()
+
+        return carry
+
+    @pl.when(has_other & (lead == 0))
+    def _():
+        lax.fori_loop(1, size, direct, 0)
+
+    def source(t):
+        return (loc + size - t) % size
+
+    def forward(t):
+        @pl.when(exporter & jnp.logical_not(straight(source(t), loc)))
+        def _():
+            forward_copy(source(t)).start()
+
+    def early(t, carry):
+        @pl.when(t > 0)
+        def _():
+            arrived(size + source(t))
+
+        @pl.when(lead == 0)
+        def _():
+            forward(t)
+
+        pair_copy(source(t)).start()
+        return carry
+
+    def late(t, carry):
+        arrived(size + source(t))
+        forward(t)
+        pair_copy(source(t)).start()
+        return carry
+
+    lax.fori_loop(0, size // 4, early, 0)
+
+    @pl.when(has_other & (lead == 1))
+    def _():
+        pl.semaphore_wait(far_sem, 1 + nearer)
+        pl.semaphore_signal(
+            all_sem, inc=1, device_id=(other, loc), device_id_type=MESH
+        )
+
+        def delayed(t, carry):
+            forward(t)
+            return carry
+
+        lax.fori_loop(1, size, direct, 0)
+        lax.fori_loop(0, size // 4, delayed, 0)
+
+    lax.fori_loop(size // 4, size, late, 0)
 
     ext[pl.ds(size, size)] = own[pl.ds(size, size)]
 
@@ -437,18 +449,42 @@
     lax.fori_loop(0, pieces, mix, 0)
     out_ref[0, loc] = res[loc]
 
-    def settle(i, carry):
+    def sent(i, carry):
         @pl.when(i != loc)
+        def _():
+            own_copy(i).wait_send()
+            ret_copy(i).wait_send()
+
+        @pl.when(has_other & exports(i) & straight(loc, i))
+        def _():
+            far_copy(i).wait_send()
+
+        @pl.when(exporter & jnp.logical_not(straight(i, loc)))
+        def _():
+            forward_copy(i).wait_send()
+
+        @pl.when(importer)
+        def _():
+            give_copy(i).wait_send()
+
+        pair_copy(i).wait_send()
+        return carry
+
+    lax.fori_loop(0, size, sent, 0)
+
+    def settle(t, carry):
+        i = turn(t)
+
+        @pl.when(t > 0)
         def _():
             pltpu.make_async_remote_copy(
                 src_ref=res.at[i],
                 dst_ref=out_ref.at[0, i],
                 send_sem=ret_send.at[i],
                 recv_sem=out_recv.at[i],
-                device_id=(grp, i),
+                device_id=(partner, loc),
                 device_id_type=MESH,
-            ).wait()
-            own_copy(i).wait_send()
+            ).wait_recv()
 
         @pl.when(has_other & exports(i))
         def _():
@@ -457,25 +493,12 @@
                 dst_ref=part.at[i],
                 send_sem=give_send.at[i],
                 recv_sem=part_recv.at[i],
-                device_id=(other, i),
+                device_id=(partner, loc),
                 device_id_type=MESH,
             ).wait_recv()
             total = out_ref[0, i].astype(jnp.float32) + part[i].astype(jnp.float32)
             out_ref[0, i] = total.astype(jnp.bfloat16)
 
-            @pl.when(straight(loc, i))
-            def _():
-                far_copy(i).wait_send()
-
-        @pl.when(exporter & jnp.logical_not(straight(i, loc)))
-        def _():
-            forward_copy(i).wait_send()
-
-        @pl.when(importer)
-        def _():
-            give_copy(i).wait_send()
-
-        pair_copy(i).wait_send()
         return carry
 
     lax.fori_loop(0, size, settle, 0)

time: 36.9 us -> 36.1 us (0.978)
  Pallas kernels: 36.1 us -> 35.3 us
    pallas_call x1, Pallas kernels: 36.1 us -> 35.3 us  [step(): pl.pallas_call(functools.partial(kernel, groups), out_shape=pltpu.VMEM((1...]
where the time goes in v4:
time: 36.1 us; the launch traced here: 36 us
  Pallas kernels  35.3 us (98%)
  local copies, waits for them, and re-layouts  0.71 us (2%)
    pallas_call x1, Pallas kernels, step(): pl.pallas_call(functools.partial(kernel, groups), out_shape=pltpu.VMEM((1...  35.3 us

profile of v4, /device:TPU:1, one launch (start us, length us, event | category | flops | bytes accessed | tf_op | source)
XLA Modules:
  0.0 36.0 jit_solution(14908968727691188717)
XLA Ops:
  0.0 35.3 %shard_map.64 = bf16[1,16,64,128]{3,2,1,0:T(8,128)(2,1)S(1)} custom-call(s32[2,16]{1,0:T(2,128)} %bitcast.1, f32[6]{0:T(128)} %occ_hbm.1, s32[6]{0:T(128)} %shift_hbm.1, bf16[1,16,3,64,128]{4,3,2,1,0:T(8,128)(2,1)} %green_hbm.1, bf16[1,16,64,128]{3,2,1,0:T(8,128)(2,1)} %sigma_hbm.1, bf16[6,1,64,128]{3,2,1,0:T(8,128)(2,1)} %coup_hbm.1), custom_call_target="tpu_custom_call" | custom-call | tf_op jit(solution)/shard_map/pallas_call | solution.py:517
  35.3 0.7 %copy.8 = bf16[1,16,64,128]{3,2,1,0:T(8,128)(2,1)} copy(bf16[1,16,64,128]{3,2,1,0:T(8,128)(2,1)S(1)} %shard_map.64) | data formatting | bytes 524288

commit v5 on v4

--- a/solution.py
+++ b/solution.py
@@ -50,7 +50,6 @@
     in_sem,
     own_send,
     far_send,
-    fwd_send,
     pair_send,
     ret_send,
     ext_recv,
@@ -58,12 +57,11 @@
     give_send,
     part_recv,
     far_sem,
-    all_sem,
 ):
     atoms, orb, lanes = sigma.shape
     size = atoms
     modes = right.shape[0]
-    chunk = 4
+    chunk = mid.shape[0]
     batch = min(4, size // 2)
     lag = batch
     run = min(RUN, size // 2)
@@ -102,22 +100,13 @@
     load_occ.start()
     load_shift.start()
 
-    def straight(source, worker):
-        rise = source % run - worker % run
-        return rise * (2 * core - 1) > 0
-
     def exports(worker):
         return worker % run // (run // 2) != core
 
-    exporter = has_other & exports(loc)
     importer = has_other & jnp.logical_not(exports(loc))
-
-    def reaches(i):
-        return straight(loc, i) | (i == loc)
 
     hi = (grp // 2) % 4
     lead = jnp.where(core == 1, jnp.where(hi == 3, 0, 1), jnp.where(hi == 0, 1, 0))
-    nearer = (core * here + (1 - core) * (run - 1 - here)) * (size // run)
     barrier = pltpu.get_barrier_semaphore()
 
     def greet(i, carry):
@@ -127,7 +116,7 @@
                 barrier, inc=1, device_id=(grp, i), device_id_type=MESH
             )
 
-        @pl.when(has_other & (lead == 1) & reaches(i))
+        @pl.when(has_other & (lead == 1))
         def _():
             pl.semaphore_signal(
                 barrier, inc=1, device_id=(other, i), device_id_type=MESH
@@ -210,15 +199,12 @@
 
     @pl.when(has_other & (lead == 0))
     def _():
-        pl.semaphore_wait(barrier, size + 1 + nearer)
+        pl.semaphore_wait(barrier, 2 * size)
 
         def answer(i, carry):
-            @pl.when(reaches(i))
-            def _():
-                pl.semaphore_signal(
-                    far_sem, inc=1, device_id=(other, i), device_id_type=MESH
-                )
-
+            pl.semaphore_signal(
+                far_sem, inc=1, device_id=(other, i), device_id_type=MESH
+            )
             return carry
 
         lax.fori_loop(0, size, answer, 0)
@@ -247,16 +233,6 @@
             send_sem=far_send.at[a],
             recv_sem=ext_recv.at[far_base + loc],
             device_id=(other, a),
-            device_id_type=MESH,
-        )
-
-    def forward_copy(j):
-        return pltpu.make_async_remote_copy(
-            src_ref=own.at[size + j],
-            dst_ref=ext.at[far_base + j],
-            send_sem=fwd_send.at[j],
-            recv_sem=ext_recv.at[far_base + j],
-            device_id=(other, loc),
             device_id_type=MESH,
         )
 
@@ -300,7 +276,7 @@
     own[size + loc] = mine[loc]
 
     def direct(t, carry):
-        @pl.when(straight(loc, turn(t)) & exports(turn(t)))
+        @pl.when(exports(turn(t)))
         def _():
             far_copy(turn(t)).start()
 
@@ -308,57 +284,35 @@
 
     @pl.when(has_other & (lead == 0))
     def _():
-        lax.fori_loop(1, size, direct, 0)
+        lax.fori_loop(1, size + 1, direct, 0)
 
     def source(t):
         return (loc + size - t) % size
 
-    def forward(t):
-        @pl.when(exporter & jnp.logical_not(straight(source(t), loc)))
-        def _():
-            forward_copy(source(t)).start()
-
     def early(t, carry):
         @pl.when(t > 0)
         def _():
             arrived(size + source(t))
 
-        @pl.when(lead == 0)
-        def _():
-            forward(t)
-
         pair_copy(source(t)).start()
         return carry
 
     def late(t, carry):
         arrived(size + source(t))
-        forward(t)
         pair_copy(source(t)).start()
         return carry
 
-    lax.fori_loop(0, size // 4, early, 0)
+    lax.fori_loop(0, size - size // 4, early, 0)
 
     @pl.when(has_other & (lead == 1))
     def _():
-        pl.semaphore_wait(far_sem, 1 + nearer)
-        pl.semaphore_signal(
-            all_sem, inc=1, device_id=(other, loc), device_id_type=MESH
-        )
-
-        def delayed(t, carry):
-            forward(t)
-            return carry
-
-        lax.fori_loop(1, size, direct, 0)
-        lax.fori_loop(0, size // 4, delayed, 0)
-
-    lax.fori_loop(size // 4, size, late, 0)
+        pl.semaphore_wait(far_sem, size)
+
+        lax.fori_loop(1, size + 1, direct, 0)
+
+    lax.fori_loop(size - size // 4, size, late, 0)
 
     ext[pl.ds(size, size)] = own[pl.ds(size, size)]
-
-    @pl.when(has_other & (lead == 0))
-    def _():
-        pl.semaphore_wait(all_sem, 1)
 
     def give_copy(i):
         return pltpu.make_async_remote_copy(
@@ -455,13 +409,9 @@
             own_copy(i).wait_send()
             ret_copy(i).wait_send()
 
-        @pl.when(has_other & exports(i) & straight(loc, i))
+        @pl.when(has_other & exports(i))
         def _():
             far_copy(i).wait_send()
-
-        @pl.when(exporter & jnp.logical_not(straight(i, loc)))
-        def _():
-            forward_copy(i).wait_send()
 
         @pl.when(importer)
         def _():
@@ -532,7 +482,7 @@
                 pltpu.VMEM((3 * size, orb, lanes), half),
                 pltpu.VMEM((modes, 2 * lanes, lanes), half),
                 pltpu.VMEM((lanes, modes * orb), half),
-                pltpu.VMEM((4, modes * orb, lanes), half),
+                pltpu.VMEM((min(8, size // 2), modes * orb, lanes), half),
                 pltpu.VMEM((size, orb, lanes), half),
                 pltpu.VMEM((size, orb, lanes), half),
                 pltpu.VMEM((size, orb, lanes), half),
@@ -541,12 +491,10 @@
                 pltpu.SemaphoreType.DMA((size,)),
                 pltpu.SemaphoreType.DMA((size,)),
                 pltpu.SemaphoreType.DMA((size,)),
-                pltpu.SemaphoreType.DMA((size,)),
                 pltpu.SemaphoreType.DMA((3 * size,)),
                 pltpu.SemaphoreType.DMA((size,)),
                 pltpu.SemaphoreType.DMA((size,)),
                 pltpu.SemaphoreType.DMA((size,)),
-                pltpu.SemaphoreType.REGULAR,
                 pltpu.SemaphoreType.REGULAR,
             ],
             compiler_params=pltpu.CompilerParams(

time: 36.1 us -> 36 us (level)
  Pallas kernels: 35.3 us -> 34.9 us
    pallas_call x1, Pallas kernels: 35.3 us -> 34.9 us  [step(): pl.pallas_call(functools.partial(kernel, groups), out_shape=pltpu.VMEM((1...]
where the time goes in v5:
time: 36 us; the launch traced here: 35.6 us
  Pallas kernels  34.9 us (97%)
  local copies, waits for them, and re-layouts  0.71 us (2%)
    pallas_call x1, Pallas kernels, step(): pl.pallas_call(functools.partial(kernel, groups), out_shape=pltpu.VMEM((1...  34.9 us

profile of v5, /device:TPU:1, one launch (start us, length us, event | category | flops | bytes accessed | tf_op | source)
XLA Modules:
  0.0 35.6 jit_solution(2631126546459362653)
XLA Ops:
  0.0 34.9 %shard_map.64 = bf16[1,16,64,128]{3,2,1,0:T(8,128)(2,1)S(1)} custom-call(s32[2,16]{1,0:T(2,128)} %bitcast.1, f32[6]{0:T(128)} %occ_hbm.1, s32[6]{0:T(128)} %shift_hbm.1, bf16[1,16,3,64,128]{4,3,2,1,0:T(8,128)(2,1)} %green_hbm.1, bf16[1,16,64,128]{3,2,1,0:T(8,128)(2,1)} %sigma_hbm.1, bf16[6,1,64,128]{3,2,1,0:T(8,128)(2,1)} %coup_hbm.1), custom_call_target="tpu_custom_call" | custom-call | tf_op jit(solution)/shard_map/pallas_call | solution.py:467
  34.9 0.7 %copy.8 = bf16[1,16,64,128]{3,2,1,0:T(8,128)(2,1)} copy(bf16[1,16,64,128]{3,2,1,0:T(8,128)(2,1)S(1)} %shard_map.64) | data formatting | bytes 524288

commit v6 on v5

--- a/solution.py
+++ b/solution.py
@@ -88,6 +88,35 @@
     load_occ = pltpu.make_async_copy(occ_hbm, occ_ref, in_sem.at[atoms + 2])
     load_shift = pltpu.make_async_copy(shift_hbm, shift_ref, in_sem.at[atoms + 3])
     load_coup = pltpu.make_async_copy(coup_hbm, coup_ref, in_sem.at[atoms + 4])
+    def exports(worker):
+        return worker % run // (run // 2) != core
+
+    importer = has_other & jnp.logical_not(exports(loc))
+
+    hi = (grp // 2) % 4
+    lead = jnp.where(core == 1, jnp.where(hi == 3, 0, 1), jnp.where(hi == 0, 1, 0))
+    barrier = pltpu.get_barrier_semaphore()
+
+    def greet(i, carry):
+        @pl.when(i != loc)
+        def _():
+            pl.semaphore_signal(
+                barrier, inc=1, device_id=(grp, i), device_id_type=MESH
+            )
+
+        @pl.when(has_other & (lead == 1))
+        def _():
+            pl.semaphore_signal(
+                barrier, inc=1, device_id=(other, i), device_id_type=MESH
+            )
+
+        return carry
+
+    lax.fori_loop(0, size, greet, 0)
+    pl.semaphore_signal(
+        barrier, inc=1, device_id=(partner, loc), device_id_type=MESH
+    )
+
     load_sigma.start()
     load_near.start()
 
@@ -99,35 +128,6 @@
     load_coup.start()
     load_occ.start()
     load_shift.start()
-
-    def exports(worker):
-        return worker % run // (run // 2) != core
-
-    importer = has_other & jnp.logical_not(exports(loc))
-
-    hi = (grp // 2) % 4
-    lead = jnp.where(core == 1, jnp.where(hi == 3, 0, 1), jnp.where(hi == 0, 1, 0))
-    barrier = pltpu.get_barrier_semaphore()
-
-    def greet(i, carry):
-        @pl.when(i != loc)
-        def _():
-            pl.semaphore_signal(
-                barrier, inc=1, device_id=(grp, i), device_id_type=MESH
-            )
-
-        @pl.when(has_other & (lead == 1))
-        def _():
-            pl.semaphore_signal(
-                barrier, inc=1, device_id=(other, i), device_id_type=MESH
-            )
-
-        return carry
-
-    lax.fori_loop(0, size, greet, 0)
-    pl.semaphore_signal(
-        barrier, inc=1, device_id=(partner, loc), device_id_type=MESH
-    )
 
     own[pl.ds(0, size)] = jnp.zeros((size, orb, lanes), own.dtype)
     own[pl.ds(2 * size, size)] = jnp.zeros((size, orb, lanes), own.dtype)

time: 36 us -> 35.9 us (level)
  no operation moved by 1% of the time
where the time goes in v6:
time: 35.9 us; the launch traced here: 35.8 us
  Pallas kernels  35.1 us (98%)
  local copies, waits for them, and re-layouts  0.71 us (2%)
    pallas_call x1, Pallas kernels, step(): pl.pallas_call(functools.partial(kernel, groups), out_shape=pltpu.VMEM((1...  35.1 us

profile of v6, /device:TPU:1, one launch (start us, length us, event | category | flops | bytes accessed | tf_op | source)
XLA Modules:
  0.0 35.8 jit_solution(16448239569603996851)
XLA Ops:
  0.0 35.1 %shard_map.64 = bf16[1,16,64,128]{3,2,1,0:T(8,128)(2,1)S(1)} custom-call(s32[2,16]{1,0:T(2,128)} %bitcast.1, f32[6]{0:T(128)} %occ_hbm.1, s32[6]{0:T(128)} %shift_hbm.1, bf16[1,16,3,64,128]{4,3,2,1,0:T(8,128)(2,1)} %green_hbm.1, bf16[1,16,64,128]{3,2,1,0:T(8,128)(2,1)} %sigma_hbm.1, bf16[6,1,64,128]{3,2,1,0:T(8,128)(2,1)} %coup_hbm.1), custom_call_target="tpu_custom_call" | custom-call | tf_op jit(solution)/shard_map/pallas_call | solution.py:467
  35.1 0.7 %copy.8 = bf16[1,16,64,128]{3,2,1,0:T(8,128)(2,1)} copy(bf16[1,16,64,128]{3,2,1,0:T(8,128)(2,1)S(1)} %shard_map.64) | data formatting | bytes 524288
